TPU v7x, 32 devices: a whole 2x2x4 slice. The times are simulated.
32 devices in a mesh: prow: 4 (over x, core), pcol: 8 (over z, y).
Axes of the slice: x: 2, y: 2, z: 4, core: 2. Of those that a mesh axis runs over, the one named last changes fastest.
Arguments:
- slab: float32 [16384, 2048], P('prow', 'pcol'), may hold values from -6 to 6
- panel: float32 [16384, 512], P(('prow', 'pcol')), may hold values from -0.25 to 0.25
- pivots: int32 [512], replicated, may hold values from 0 to 16383, as said below
- inv_lower: float32 [512, 512], replicated, as said below
- inv_upper: float32 [512, 512], replicated, as said below
Outputs:
- updated: float32 [16384, 2048], P('prow', 'pcol')
Inputs may be any that keep to these rules, and one draw needn't show every extreme that they name: `pivots`: 512 distinct row indices. `inv_lower`: unit lower triangular. `inv_upper`: upper triangular with a positive diagonal.
All inputs are finite; a program needn't handle non-finite values.
Results may differ from a plain program's by a relative error of at most 0.000061.
Values sent between devices are 32-bit elements; how exact they have to be, the bound alone decides.
A program may use at most 64 MiB of HBM per device.

v0:
```python
import jax
import jax.numpy as jnp
from jax import lax
from jax.sharding import PartitionSpec as P


def local(slab, panel, pivots, inv_lower, inv_upper):
    row_count = slab.shape[0]
    first_row = lax.axis_index("prow") * row_count
    local_index = pivots - first_row
    inside = (local_index >= 0) & (local_index < row_count)
    safe_index = jnp.where(inside, local_index, 0)
    picked = jnp.where(inside[:, None], jnp.take(slab, safe_index, axis=0), 0.0)
    pivot_rows = lax.psum(picked, "prow")
    upper_block = jnp.dot(
        inv_lower, pivot_rows, precision=lax.Precision.HIGHEST, preferred_element_type=jnp.float32
    )
    own_lower = jnp.dot(
        panel, inv_upper, precision=lax.Precision.HIGHEST, preferred_element_type=jnp.float32
    )
    product = jnp.dot(
        lax.all_gather(own_lower, "pcol", axis=0, tiled=True),
        upper_block,
        precision=lax.Precision.HIGHEST,
        preferred_element_type=jnp.float32,
    )
    updated = slab - product
    target = jnp.where(inside, local_index, row_count)
    return updated.at[target].set(upper_block, mode="drop")


def solution(mesh):
    return jax.shard_map(
        local,
        mesh=mesh,
        in_specs=(P("prow", "pcol"), P(("prow", "pcol"), None), P(), P(), P()),
        out_specs=P("prow", "pcol"),
        check_vma=False,
    )
```

profile of v0, /device:TPU:0, one launch (start us, length us, event | category | flops | bytes accessed | tf_op | source)
XLA Modules:
  0.0 168.0 jit_solution(13603019011698801581)
XLA Ops:
  7.4 0.0 copy-start
  7.4 0.0 copy-start.1
  7.4 0.0 all-reduce.2.cloned.1.call-start
  7.4 0.8 compare_and_fusion
  8.2 0.0 copy-start.3
  8.2 3.8 %gather_fusion = f32[512,256]{1,0:T(8,128)S(1)} fusion(f32[4096,256]{1,0:T(8,128)} %param.5, s32[1024]{0:T(1024)S(1)} %pad_clamp_fusion), kind=kCustom, calls=%fused_computation | custom fusion | bytes 1050624 | tf_op jit(solution)/shard_map/jit(_take)/gather | solution.py:13
  12.0 1.0 select_select_fusion
  13.0 0.0 copy-start.2
  13.0 0.0 all-reduce.2.cloned.1.call-update
  13.1 0.0 all-gather.2.cloned.1.call-start
  13.1 0.0 copy-done
  13.1 0.0 copy-done.1
  13.1 2.8 %fusion = f32[512,512]{1,0:T(8,128)} fusion(f32[512,512]{1,0:T(8,128)S(1)} %copy-done, f32[512,512]{1,0:T(8,128)S(1)} %copy-done.1), kind=kOutput, calls=%fused_computation.9 | convolution fusion | flops 1610612736 | bytes 3145728 | tf_op jit(solution)/shard_map/dot_general | solution.py:18
  16.0 0.0 all-gather.2.cloned.1.call-update
  16.0 0.0 copy-done.3
  16.0 33.5 %all-reduce.2.cloned.1.call-done = f32[512,256]{1,0:T(8,128)} async-done(((f32[512,256]{1,0:T(8,128)}), f32[512,256]{1,0:T(8,128)}) %all-reduce.2.cloned.1.call-update) | async-done | bytes 524304 | tf_op jit(solution)/shard_map/psum | solution.py:14
  49.5 0.0 copy-done.2
  49.5 2.9 %fusion.1 = f32[256,512]{1,0:T(8,128)S(1)} fusion(f32[512,256]{1,0:T(8,128)} %all-reduce.2.cloned.1.call-done, f32[512,512]{1,0:T(8,128)S(1)} %copy-done.2), kind=kOutput, calls=%fused_computation.10 | convolution fusion | flops 805306368 | bytes 2097152 | tf_op jit(solution)/shard_map/dot_general | solution.py:15
  52.4 0.2 copy.6
  52.6 90.4 %all-gather.2.cloned.1.call-done = f32[4096,512]{1,0:T(8,128)} async-done(((f32[512,512]{1,0:T(8,128)}), f32[4096,512]{1,0:T(8,128)}) %all-gather.2.cloned.1.call-update) | async-done | bytes 8388624 | tf_op jit(solution)/shard_map/all_gather | solution.py:22
  143.0 11.2 %convolution_subtract_fusion = f32[4096,256]{1,0:T(8,128)} fusion(f32[4096,256]{1,0:T(8,128)} %param.5, f32[4096,512]{1,0:T(8,128)} %all-gather.2.cloned.1.call-done, f32[256,512]{1,0:T(8,128)S(1)} %fusion.1), kind=kOutput, calls=%fused_computation.2 | convolution fusion | flops 6443499520 | bytes 17301504 | tf_op jit(solution)/shard_map/dot_general | solution.py:21
  154.2 6.4 %scatter_fusion = f32[4096,256]{1,0:T(8,128)} fusion(f32[4096,256]{1,0:T(8,128)} %convolution_subtract_fusion, s32[512]{0:T(512)S(1)} %compare_select_fusion, f32[512,256]{1,0:T(8,128)S(1)} %copy.6), kind=kCustom, calls=%fused_computation.1 | custom fusion | bytes 1574912 | tf_op jit(solution)/shard_map/scatter | solution.py:29
  (2 shorter events, 0.0 us)
Async XLA Ops:
  7.4 5.8 %copy-start = (f32[512,512]{1,0:T(8,128)S(1)}, f32[512,512]{1,0:T(8,128)}, u32[]{:S(2)}) copy-start(f32[512,512]{1,0:T(8,128)} %param.6) | copy-start | bytes 3145732
  7.4 5.8 %copy-start.1 = (f32[512,512]{1,0:T(8,128)S(1)}, f32[512,512]{1,0:T(8,128)}, u32[]{:S(2)}) copy-start(f32[512,512]{1,0:T(8,128)} %param.9) | copy-start | bytes 3145732
  7.4 42.1 %all-reduce.2.cloned.1.call-start = ((), (), s32[]{:S(2)}) async-start(), calls=%async_computation.1 | async-start | bytes 1048576 | tf_op jit(solution)/shard_map/psum | solution.py:14
  8.2 7.8 %copy-start.3 = (s32[512]{0:T(512)S(1)}, s32[512]{0:T(512)}, u32[]{:S(2)}) copy-start(s32[512]{0:T(512)} %param.7) | copy-start | bytes 6148
  13.0 36.4 %copy-start.2 = (f32[512,512]{1,0:T(8,128)S(1)}, f32[512,512]{1,0:T(8,128)}, u32[]{:S(2)}) copy-start(f32[512,512]{1,0:T(8,128)} %param.8) | copy-start | bytes 3145732
  13.1 129.9 %all-gather.2.cloned.1.call-start = ((), (), s32[]{:S(2)}) async-start(), calls=%async_computation | async-start | bytes 9437184 | tf_op jit(solution)/shard_map/all_gather | solution.py:22
Sparse Core Ops, SparseCore 0:
  13.2 36.2 all-reduce.1
Sparse Core Ops, SparseCore 1:
  16.1 126.9 all-gather.1
where the time goes:
time: 168 us
  waiting for transfers between devices  124 us (74%)
  matrix products  16.9 us (10%)
  between operations  14.9 us (9%)
  local copies, waits for them, and re-layouts  10.4 us (6%)
  other arithmetic  1.89 us (1%)
    all_gather x1, waiting for transfers between devices, local(): lax.all_gather(own_lower, 'pcol', axis=0, tiled=True)  90.4 us
    psum x1, waiting for transfers between devices, local(): pivot_rows = lax.psum(picked, 'prow')  33.5 us
    dot_general x1, matrix products, local(): jnp.dot(lax.all_gather(own_lower, 'pcol', axis=0, tiled=True), upper_bloc...  11.2 us
    scatter x1, local copies, waits for them, and re-layouts, local(): return updated.at[target].set(upper_block, mode='drop')  6.39 us
    gather x1, local copies, waits for them, and re-layouts, local(): picked = jnp.where(inside[:, None], jnp.take(slab, safe_index, axis=0), 0.0)  3.76 us
  transfers between devices with their start and end apart: 2, of which 2 were waited for; matrix products, arithmetic and copies ran while one was open for 4% of the time, Pallas kernels for 0%

commit v1 on v0

--- a/solution.py
+++ b/solution.py
@@ -11,7 +11,7 @@
     inside = (local_index >= 0) & (local_index < row_count)
     safe_index = jnp.where(inside, local_index, 0)
     picked = jnp.where(inside[:, None], jnp.take(slab, safe_index, axis=0), 0.0)
-    pivot_rows = lax.psum(picked, "prow")
+    pivot_rows = jnp.sum(lax.all_gather(picked, "prow"), axis=0)
     upper_block = jnp.dot(
         inv_lower, pivot_rows, precision=lax.Precision.HIGHEST, preferred_element_type=jnp.float32
     )

time: 168 us -> 189 us (1.12)
  waiting for transfers between devices: 124 us -> 145 us
    psum x1 -> x0, waiting for transfers between devices: 33.5 us -> none  [local(): pivot_rows = lax.psum(picked, 'prow')]
    all_gather x1, waiting for transfers between devices: 90.4 us -> 123 us  [local(): lax.all_gather(own_lower, 'pcol', axis=0, tiled=True)]
    all_gather x0 -> x1, waiting for transfers between devices: none -> 22.5 us  [local(): pivot_rows = jnp.sum(lax.all_gather(picked, 'prow'), axis=0)]
where the time goes in v1:
time: 189 us
  waiting for transfers between devices  145 us (77%)
  matrix products  15.9 us (8%)
  between operations  13.5 us (7%)
  local copies, waits for them, and re-layouts  10.4 us (6%)
  other arithmetic  3.67 us (2%)
    all_gather x1, waiting for transfers between devices, local(): lax.all_gather(own_lower, 'pcol', axis=0, tiled=True)  123 us
    all_gather x1, waiting for transfers between devices, local(): pivot_rows = jnp.sum(lax.all_gather(picked, 'prow'), axis=0)  22.5 us
    dot_general x1, matrix products, local(): jnp.dot(lax.all_gather(own_lower, 'pcol', axis=0, tiled=True), upper_bloc...  11.2 us
    scatter x1, local copies, waits for them, and re-layouts, local(): return updated.at[target].set(upper_block, mode='drop')  6.39 us
  transfers between devices with their start and end apart: 2, of which 2 were waited for; matrix products, arithmetic and copies ran while one was open for 4% of the time, Pallas kernels for 0%

profile of v1, /device:TPU:0, one launch (start us, length us, event | category | flops | bytes accessed | tf_op | source)
XLA Modules:
  0.0 188.7 jit_solution(8089885801633029652)
XLA Ops:
  6.5 0.0 copy-start
  6.5 0.0 copy-start.1
  6.5 0.0 all-gather.5.cloned.1.call-start
  6.5 0.8 compare_and_fusion
  7.4 0.0 copy-start.3
  7.4 3.8 %gather_fusion = f32[512,256]{1,0:T(8,128)S(1)} fusion(f32[4096,256]{1,0:T(8,128)} %param.5, s32[1024]{0:T(1024)S(1)} %pad_clamp_fusion), kind=kCustom, calls=%fused_computation | custom fusion | bytes 1050624 | tf_op jit(solution)/shard_map/jit(_take)/gather | solution.py:13
  11.2 1.0 fusion
  12.2 0.0 copy-start.2
  12.2 0.0 all-gather.5.cloned.1.call-update
  12.2 0.0 all-gather.3.cloned.1.call-start
  12.3 0.0 copy-done
  12.3 0.0 copy-done.1
  12.3 2.8 %fusion.1 = f32[512,512]{1,0:T(8,128)} fusion(f32[512,512]{1,0:T(8,128)S(1)} %copy-done, f32[512,512]{1,0:T(8,128)S(1)} %copy-done.1), kind=kOutput, calls=%fused_computation.10 | convolution fusion | flops 1610612736 | bytes 3145728 | tf_op jit(solution)/shard_map/dot_general | solution.py:18
  15.1 0.0 all-gather.3.cloned.1.call-update
  15.1 0.0 copy-done.3
  15.2 22.5 %all-gather.5.cloned.1.call-done = f32[4,512,256]{2,1,0:T(8,128)} async-done(((f32[1,512,256]{2,1,0:T(8,128)}), f32[4,512,256]{2,1,0:T(8,128)}) %all-gather.5.cloned.1.call-update) | async-done | bytes 2097168 | tf_op jit(solution)/shard_map/all_gather | solution.py:14
  37.7 1.8 reduce_sum.9
  39.5 0.0 copy-done.2
  39.5 1.9 fusion.2
  41.3 0.2 copy.7
  41.5 122.8 %all-gather.3.cloned.1.call-done = f32[4096,512]{1,0:T(8,128)} async-done(((f32[512,512]{1,0:T(8,128)}), f32[4096,512]{1,0:T(8,128)}) %all-gather.3.cloned.1.call-update) | async-done | bytes 8388624 | tf_op jit(solution)/shard_map/all_gather | solution.py:22
  164.3 11.2 %convolution_subtract_fusion = f32[4096,256]{1,0:T(8,128)} fusion(f32[4096,256]{1,0:T(8,128)} %param.5, f32[4096,512]{1,0:T(8,128)} %all-gather.3.cloned.1.call-done, f32[256,512]{1,0:T(8,128)S(1)} %fusion.2), kind=kOutput, calls=%fused_computation.2 | convolution fusion | flops 6443499520 | bytes 17301504 | tf_op jit(solution)/shard_map/dot_general | solution.py:21
  175.5 6.4 %scatter_fusion = f32[4096,256]{1,0:T(8,128)} fusion(f32[4096,256]{1,0:T(8,128)} %convolution_subtract_fusion, s32[512]{0:T(512)S(1)} %compare_select_fusion, f32[512,256]{1,0:T(8,128)S(1)} %copy.7), kind=kCustom, calls=%fused_computation.1 | custom fusion | bytes 1574912 | tf_op jit(solution)/shard_map/scatter | solution.py:29
  (2 shorter events, 0.0 us)
Async XLA Ops:
  6.5 5.7 %copy-start = (f32[512,512]{1,0:T(8,128)S(1)}, f32[512,512]{1,0:T(8,128)}, u32[]{:S(2)}) copy-start(f32[512,512]{1,0:T(8,128)} %param.6) | copy-start | bytes 3145732
  6.5 5.8 %copy-start.1 = (f32[512,512]{1,0:T(8,128)S(1)}, f32[512,512]{1,0:T(8,128)}, u32[]{:S(2)}) copy-start(f32[512,512]{1,0:T(8,128)} %param.9) | copy-start | bytes 3145732
  6.5 31.1 %all-gather.5.cloned.1.call-start = ((), (), s32[]{:S(2)}) async-start(), calls=%async_computation.1 | async-start | bytes 2621440 | tf_op jit(solution)/shard_map/all_gather | solution.py:14
  7.4 7.8 %copy-start.3 = (s32[512]{0:T(512)S(1)}, s32[512]{0:T(512)}, u32[]{:S(2)}) copy-start(s32[512]{0:T(512)} %param.7) | copy-start | bytes 6148
  12.2 27.3 %copy-start.2 = (f32[512,512]{1,0:T(8,128)S(1)}, f32[512,512]{1,0:T(8,128)}, u32[]{:S(2)}) copy-start(f32[512,512]{1,0:T(8,128)} %param.8) | copy-start | bytes 3145732
  12.2 152.1 %all-gather.3.cloned.1.call-start = ((), (), s32[]{:S(2)}) async-start(), calls=%async_computation | async-start | bytes 9437184 | tf_op jit(solution)/shard_map/all_gather | solution.py:22
Sparse Core Ops, SparseCore 0:
  12.4 25.2 all-gather.4
  39.8 124.4 all-gather.2

commit v2 on v0

--- a/solution.py
+++ b/solution.py
@@ -19,7 +19,9 @@
         panel, inv_upper, precision=lax.Precision.HIGHEST, preferred_element_type=jnp.float32
     )
     product = jnp.dot(
-        lax.all_gather(own_lower, "pcol", axis=0, tiled=True),
+        jnp.concatenate(
+            lax.all_to_all(jnp.stack([own_lower] * lax.axis_size("pcol")), "pcol", 0, 0), axis=0
+        ),
         upper_block,
         precision=lax.Precision.HIGHEST,
         preferred_element_type=jnp.float32,

time: 168 us -> 231 us (1.38)
  waiting for transfers between devices: 124 us -> 175 us
  starting transfers between devices: 0.05 us -> 7.48 us
  local copies, waits for them, and re-layouts: 10.4 us -> 16 us
    all_to_all x0 -> x1, waiting for transfers between devices: none -> 140 us  [local(): lax.all_to_all(jnp.stack([own_lower] * lax.axis_size('pcol')), 'pcol', 0, 0)]
    all_gather x1 -> x0, waiting for transfers between devices: 90.4 us -> none  [local(): lax.all_gather(own_lower, 'pcol', axis=0, tiled=True)]
    all_to_all x0 -> x1, starting transfers between devices: none -> 7.44 us  [local(): lax.all_to_all(jnp.stack([own_lower] * lax.axis_size('pcol')), 'pcol', 0, 0)]
    another operation x0 -> x1, local copies, waits for them, and re-layouts: none -> 4.3 us  [local(): jnp.stack([own_lower] * lax.axis_size('pcol'))]
  transfers between devices with their start and end apart: 2 -> 2, of which waited for: 2 -> 2; matrix products, arithmetic and copies ran while one was open for 4% -> 3% of each run, Pallas kernels for 0% -> 0%
where the time goes in v2:
time: 231 us; the launch traced here: 230 us
  waiting for transfers between devices  175 us (76%)
  matrix products  17.2 us (7%)
  local copies, waits for them, and re-layouts  16 us (7%)
  between operations  13.5 us (6%)
  starting transfers between devices  7.48 us (3%)
    all_to_all x1, waiting for transfers between devices, local(): lax.all_to_all(jnp.stack([own_lower] * lax.axis_size('pcol')), 'pcol', 0, 0)  140 us
    psum x1, waiting for transfers between devices, local(): pivot_rows = lax.psum(picked, 'prow')  35 us
    dot_general x1, matrix products, local(): jnp.dot(jnp.concatenate(lax.all_to_all(jnp.stack([own_lower] * lax.axis_s...  11.2 us
    all_to_all x1, starting transfers between devices, local(): lax.all_to_all(jnp.stack([own_lower] * lax.axis_size('pcol')), 'pcol', 0, 0)  7.44 us
    scatter x1, local copies, waits for them, and re-layouts, local(): return updated.at[target].set(upper_block, mode='drop')  6.39 us
  transfers between devices with their start and end apart: 2, of which 2 were waited for; matrix products, arithmetic and copies ran while one was open for 3% of the time, Pallas kernels for 0%

profile of v2, /device:TPU:0, one launch (start us, length us, event | category | flops | bytes accessed | tf_op | source)
XLA Modules:
  0.0 230.2 jit_solution(7944536714986802093)
XLA Ops:
  6.5 0.0 copy-start
  6.5 1.2 copy-done
  7.8 3.1 %fusion = f32[512,512]{1,0:T(8,128)S(1)} fusion(f32[512,512]{1,0:T(8,128)S(1)} %copy-done, f32[512,512]{1,0:T(8,128)} %param.9), kind=kOutput, calls=%fused_computation.9 | convolution fusion | flops 1610612736 | bytes 3145728 | tf_op jit(solution)/shard_map/dot_general | solution.py:18
  10.8 4.3 %stack.2 = f32[8,512,512]{2,1,0:T(8,128)} broadcast(f32[512,512]{1,0:T(8,128)S(1)} %fusion), dimensions={1,2} | broadcast | bytes 9437184 | tf_op jit(solution)/shard_map/stack | solution.py:23
  15.1 0.0 copy-start.2
  15.1 7.4 %all-to-all-start = ((f32[8,512,512]{2,1,0:T(8,128)}), f32[8,512,512]{2,1,0:T(8,128)}, u32[]{:S(2)}, u32[]{:S(2)}) async-start(f32[8,512,512]{2,1,0:T(8,128)} %stack.2), calls=%async_computation | async-start | bytes 16777216 | tf_op jit(solution)/shard_map/all_to_all | solution.py:23
  22.6 0.0 copy-start.1
  22.6 0.0 all-reduce.2.cloned.1.call-start
  22.6 0.0 copy-done.2
  22.7 3.8 %gather_fusion = f32[512,256]{1,0:T(8,128)S(1)} fusion(f32[4096,256]{1,0:T(8,128)} %param.5, s32[1024]{0:T(1024)S(1)} %pad_clamp_fusion), kind=kCustom, calls=%fused_computation | custom fusion | bytes 1050624 | tf_op jit(solution)/shard_map/jit(_take)/gather | solution.py:13
  26.5 1.0 select_select_fusion
  27.5 0.0 all-reduce.2.cloned.1.call-update
  27.6 35.0 %all-reduce.2.cloned.1.call-done = f32[512,256]{1,0:T(8,128)} async-done(((f32[512,256]{1,0:T(8,128)}), f32[512,256]{1,0:T(8,128)}) %all-reduce.2.cloned.1.call-update) | async-done | bytes 524304 | tf_op jit(solution)/shard_map/psum | solution.py:14
  62.6 0.0 copy-done.1
  62.6 2.9 %fusion.1 = f32[256,512]{1,0:T(8,128)S(1)} fusion(f32[512,256]{1,0:T(8,128)} %all-reduce.2.cloned.1.call-done, f32[512,512]{1,0:T(8,128)S(1)} %copy-done.1), kind=kOutput, calls=%fused_computation.10 | convolution fusion | flops 805306368 | bytes 2097152 | tf_op jit(solution)/shard_map/dot_general | solution.py:15
  65.5 0.2 copy.6
  65.7 140.1 %all-to-all-done = f32[8,512,512]{2,1,0:T(8,128)} async-done(((f32[8,512,512]{2,1,0:T(8,128)}), f32[8,512,512]{2,1,0:T(8,128)}, u32[]{:S(2)}, u32[]{:S(2)}) %all-to-all-start) | async-done | bytes 8388640 | tf_op jit(solution)/shard_map/all_to_all | solution.py:23
  205.7 11.2 %convolution_subtract_fusion = f32[4096,256]{1,0:T(8,128)} fusion(f32[4096,256]{1,0:T(8,128)} %param.5, f32[4096,512]{1,0:T(8,128)} %bitcast, f32[256,512]{1,0:T(8,128)S(1)} %fusion.1), kind=kOutput, calls=%fused_computation.2 | convolution fusion | flops 6443499520 | bytes 17301504 | tf_op jit(solution)/shard_map/dot_general | solution.py:21
  216.9 6.4 %scatter_fusion = f32[4096,256]{1,0:T(8,128)} fusion(f32[4096,256]{1,0:T(8,128)} %convolution_subtract_fusion, s32[512]{0:T(512)S(1)} %compare_select_fusion, f32[512,256]{1,0:T(8,128)S(1)} %copy.6), kind=kCustom, calls=%fused_computation.1 | custom fusion | bytes 1574912 | tf_op jit(solution)/shard_map/scatter | solution.py:31
  (3 shorter events, 0.0 us)
Async XLA Ops:
  6.5 1.2 copy-start
  15.1 7.5 %copy-start.2 = (s32[512]{0:T(512)S(1)}, s32[512]{0:T(512)}, u32[]{:S(2)}) copy-start(s32[512]{0:T(512)} %param.7) | copy-start | bytes 6148
  15.1 190.6 %all-to-all-start = ((f32[8,512,512]{2,1,0:T(8,128)}), f32[8,512,512]{2,1,0:T(8,128)}, u32[]{:S(2)}, u32[]{:S(2)}) async-start(f32[8,512,512]{2,1,0:T(8,128)} %stack.2), calls=%async_computation | async-start | bytes 16777216 | tf_op jit(solution)/shard_map/all_to_all | solution.py:23
  22.6 40.0 %copy-start.1 = (f32[512,512]{1,0:T(8,128)S(1)}, f32[512,512]{1,0:T(8,128)}, u32[]{:S(2)}) copy-start(f32[512,512]{1,0:T(8,128)} %param.8) | copy-start | bytes 3145732
  22.6 40.0 %all-reduce.2.cloned.1.call-start = ((), (), s32[]{:S(2)}) async-start(), calls=%async_computation.1 | async-start | bytes 1048576 | tf_op jit(solution)/shard_map/psum | solution.py:14
Sparse Core Ops, SparseCore 0:
  27.7 34.8 all-reduce.1
